TPU v7x, 32 devices: a whole 2x2x4 slice. The times are simulated.
32 devices in a mesh: seq: 2 (over x), mp: 4 (over y, core), dp: 4 (over z).
Axes of the slice: x: 2, y: 2, z: 4, core: 2. Of those that a mesh axis runs over, the one named last changes fastest.
Arguments:
- tokens: bfloat16 [16384, 2048], P(('dp', 'seq'), 'mp'), parts along dimension 0, may hold values from -6 to 6
- w_query: bfloat16 [2048, 2048], P(None, 'mp'), may hold values from -0.125 to 0.125
- w_key: bfloat16 [2048, 2048], P(None, 'mp'), may hold values from -0.125 to 0.125
- w_value: bfloat16 [2048, 2048], P(None, 'mp'), may hold values from -0.125 to 0.125
- w_gate: bfloat16 [2048, 2048], P(None, 'mp'), may hold values from -0.125 to 0.125
- decay_exponent: int32 [16], P('mp'), may hold values from 5 to 16
- forget: float32 [16384, 16], P(('dp', 'seq'), 'mp'), parts along dimension 0, may hold values from 0 to 0.69
- norm_gain: float32 [2048], replicated, may hold values from 0.1 to 1.9
Outputs:
- retained: bfloat16 [16384, 2048], P(('dp', 'seq', 'mp')), parts along dimension 0
There are 4 independent parts, one for each index of `dp`. A program takes and returns all parts, laid end to end along the dimension named above; an argument that names none is the same for every part. Nothing has to cross between parts.
All inputs are finite; a program needn't handle non-finite values.
Results may differ from a plain program's by a relative error of at most 0.015.
Values may be sent and summed in bfloat16 or wider, within the bound.
No kernel may reach another device: no remote copies, remote signals or barrier semaphores. Data moves between devices by JAX's collectives and lax.ppermute only.
A program may use at most 64 MiB of HBM per device.

v0:
```python
import jax
import jax.numpy as jnp
from jax import lax
from jax.sharding import PartitionSpec as P

DH = 128


def carried_in(shard, axis, join, neutral):
    place = lax.axis_index(axis)
    gathered = jax.tree.map(
        lambda a, kind: lax.all_gather(a.astype(kind), axis), shard, (jnp.bfloat16, jnp.bfloat16)
    )
    state = jax.tree.map(lambda a, e: jnp.zeros_like(a) + jnp.asarray(e, a.dtype), shard, neutral)

    def one(hop, state):
        return join(
            state,
            jax.tree.map(
                lambda a, own: lax.dynamic_index_in_dim(a, hop, 0, False).astype(own.dtype),
                gathered,
                shard,
            ),
        )

    return lax.fori_loop(0, place, one, state)


def run_blocks(queries, key_rows, values, logdecay, head_count, head_width):
    seq_rows = queries.shape[0]
    block_rows = 512
    block_count = seq_rows // block_rows

    def shaped(source):
        return source.reshape(block_count, block_rows, head_count, head_width)

    decays = logdecay.reshape(block_count, block_rows, head_count)
    position = lax.broadcasted_iota(jnp.int32, (block_rows, block_rows), 0)
    earlier = lax.broadcasted_iota(jnp.int32, (block_rows, block_rows), 1)
    causal = position >= earlier

    def advance(carried, pieces):
        kv_state, offset = carried
        query_blk, key_blk, value_blk, decay_blk = pieces
        running = jnp.cumsum(decay_blk, axis=0)
        heads_first = running.T
        log_gap = heads_first[:, :, None] - heads_first[:, None, :]
        decay_mask = jnp.where(causal[None], jnp.exp(jnp.where(causal[None], log_gap, 0.0)), 0.0)
        scores = jnp.einsum("tha,sha->hts", query_blk, key_blk, preferred_element_type=jnp.float32)
        scores = (scores * decay_mask).astype(jnp.bfloat16)
        inner = jnp.einsum("hts,shb->thb", scores, value_blk, preferred_element_type=jnp.float32)
        query_float = query_blk.astype(jnp.float32)
        earlier_part = jnp.einsum(
            "tha,hab->thb",
            query_float * jnp.exp(running)[:, :, None],
            kv_state,
            precision=lax.Precision.HIGHEST,
        )
        query_device = query_float * jnp.exp(running + offset[None, :])[:, :, None]
        key_scaled = key_blk.astype(jnp.float32) * jnp.exp(running[-1:] - running)[:, :, None]
        kv_state = jnp.exp(running[-1])[:, None, None] * kv_state + jnp.einsum(
            "sha,shb->hab",
            key_scaled,
            value_blk.astype(jnp.float32),
            precision=lax.Precision.HIGHEST,
        )
        return ((kv_state, offset + running[-1]), (inner + earlier_part, query_device))

    initial = (
        jnp.zeros((head_count, head_width, head_width), jnp.float32),
        jnp.zeros((head_count,), jnp.float32),
    )
    final, outputs = lax.scan(
        advance, initial, (shaped(queries), shaped(key_rows), shaped(values), decays)
    )
    local_part = outputs[0].reshape(seq_rows, head_count, head_width)
    query_device = outputs[1].reshape(seq_rows, head_count, head_width)
    return (local_part, query_device, final[0], final[1])


def combine_states(before, after):
    return (before[0] * after[0], after[0][:, None, None] * before[1] + after[1])


def body(tokens, w_query, w_key, w_value, w_gate, decay_exponent, forget, norm_gain):
    seq_rows = tokens.shape[0]
    local_width = w_query.shape[1]
    head_count = decay_exponent.shape[0]
    head_width = local_width // head_count
    empty = jnp.zeros((seq_rows, local_width), jnp.float32)
    summed = (empty, empty, empty, empty)
    piece = lax.all_gather(tokens, "mp", axis=1, tiled=True)
    results = []
    for weight, partial_value in zip((w_query, w_key, w_value, w_gate), summed):
        results.append(jnp.dot(piece, weight, preferred_element_type=jnp.float32))
    projected = tuple(results)
    queries = projected[0].astype(jnp.bfloat16)
    key_rows = (projected[1] * DH ** (-0.5)).astype(jnp.bfloat16)
    values = projected[2].astype(jnp.bfloat16)
    gate = projected[3].astype(jnp.bfloat16)
    rate = jnp.log1p(-jnp.exp2(-decay_exponent.astype(jnp.float32)))
    logdecay = rate[None, :] - forget
    local_part, query_device, own_state, own_total = run_blocks(
        queries, key_rows, values, logdecay, head_count, head_width
    )
    prefix = carried_in(
        (jnp.exp(own_total), own_state),
        "seq",
        combine_states,
        (jnp.ones_like(own_total), jnp.zeros_like(own_state)),
    )
    incoming = prefix[1]
    from_before = jnp.einsum(
        "tha,hab->thb", query_device, incoming, precision=lax.Precision.HIGHEST
    )
    output = (local_part + from_before).astype(jnp.bfloat16).reshape(seq_rows, local_width)
    moved_output, moved_gate = (
        lax.all_to_all(output, "mp", split_axis=0, concat_axis=1, tiled=True),
        lax.all_to_all(gate, "mp", split_axis=0, concat_axis=1, tiled=True),
    )
    output_float = moved_output.astype(jnp.float32)
    rstd = lax.rsqrt(jnp.mean(output_float * output_float, axis=1) + 1e-06)
    gated = (
        jax.nn.silu(moved_gate.astype(jnp.float32))
        * output_float
        * rstd[:, None]
        * norm_gain[None, :]
    )
    return gated.astype(jnp.bfloat16)


def solution(mesh):
    placed = (
        P(("dp", "seq"), "mp"),
        P(None, "mp"),
        P(None, "mp"),
        P(None, "mp"),
        P(None, "mp"),
        P("mp"),
        P(("dp", "seq"), "mp"),
        P(),
    )
    return jax.shard_map(
        body, mesh=mesh, in_specs=placed, out_specs=P(("dp", "seq", "mp"), None), check_vma=False
    )
```

profile of v0, /device:TPU:0, one launch (start us, length us, event | category | flops | bytes accessed | tf_op | source)
XLA Modules:
  0.0 337.5 jit_solution(5486481289894038509)
XLA Ops:
  7.3 1.2 dynamic-slice
  10.7 59.2 %all-gather.4.cloned.1.call-done = bf16[2048,2048]{1,0:T(8,128)(2,1)} async-done(((bf16[2048,512]{1,0:T(8,128)(2,1)}), bf16[2048,2048]{1,0:T(8,128)(2,1)}) %all-gather.4.cloned.1.call-update) | async-done | bytes 8388624 | tf_op jit(solution)/shard_map/all_gather | solution.py:92
  69.9 9.1 %convolution_convert_fusion = bf16[2048,512]{1,0:T(8,128)(2,1)} fusion(bf16[2048,2048]{1,0:T(8,128)(2,1)} %all-gather.4.cloned.1.call-done, bf16[2048,512]{1,0:T(8,128)(2,1)S(1)} %copy-done), kind=kOutput, calls=%fused_computation.48 | convolution fusion | flops 4296015872 | bytes 12582912 | tf_op jit(solution)/shard_map/dot_general | solution.py:95
  79.0 4.0 %reshape.90 = bf16[4,512,4,128]{3,2,1,0:T(4,128)(2,1)} reshape(bf16[2048,512]{1,0:T(8,128)(2,1)} %convolution_convert_fusion) | data formatting | bytes 4194304 | tf_op jit(solution)/shard_map/reshape | solution.py:35
  83.0 8.5 %convolution_convert_fusion.1 = bf16[2048,512]{1,0:T(8,128)(2,1)S(1)} fusion(bf16[2048,2048]{1,0:T(8,128)(2,1)} %all-gather.4.cloned.1.call-done, bf16[2048,512]{1,0:T(8,128)(2,1)} %param.15), kind=kOutput, calls=%fused_computation.49 | convolution fusion | flops 4296015872 | bytes 12582912 | tf_op jit(solution)/shard_map/dot_general | solution.py:95
  91.5 2.1 reshape.89
  93.6 8.5 %multiply_convert_fusion.2 = bf16[2048,512]{1,0:T(8,128)(2,1)S(1)} fusion(bf16[2048,2048]{1,0:T(8,128)(2,1)} %all-gather.4.cloned.1.call-done, bf16[2048,512]{1,0:T(8,128)(2,1)} %param.14), kind=kOutput, calls=%fused_computation.47 | convolution fusion | flops 4297064448 | bytes 12582912 | tf_op jit(solution)/shard_map/dot_general | solution.py:95
  102.1 2.0 reshape.88
  104.1 137.0 %while.31 = (s32[]{:T(128)}, f32[4,128,128]{2,1,0:T(8,128)S(1)}, f32[4]{0:T(128)S(1)}, f32[4,512,4,128]{1,0,3,2:T(4,128)}, f32[4,512,4,128]{3,1,0,2:T(8,128)}, /...) while((s32[]{:T(128)}, f32[4,128,128]{2,1,0:T(8,128)S(1)}, ...), condition=%wide.region_3.4_spmd.clone.clone, body=%wide.region_0.3_spmd.clone.clone.sunk | while | flops 1350045696 | bytes 18760368 | solution.py:73
  107.4 1.8 constant_dynamic-slice_fusion.6
  109.1 2.0 fusion.48
  111.1 1.4 fusion.49
  112.5 2.4 convolution_add_fusion.2
  116.0 21.0 %dynamic_update_slice.15 = f32[4,512,4,128]{1,0,3,2:T(4,128)} dynamic-update-slice(f32[4,512,4,128]{1,0,3,2:T(4,128)} %get-tuple-element.371, f32[1,512,4,128]{1,0,3,2:T(1,128)S(1)} %copy.143, s32[]{:T(128)S(6)} %copy.151, s32[]{:T(128)} %constant.52.clone.1..sunk.1, s32[]{:T(128)} %constant.52.clone.1..sunk.1, s32[]{:T(128)} %constant.52.clone.1..sunk.1) | dynamic-update-slice | bytes 2097156 | tf_op jit(solution)/shard_map/while/body/jit(dynamic_update_index_in_dim)/dynamic_update_slice | solution.py:73
  137.0 1.3 bitcast_dynamic-update-slice_fusion.2
  141.6 1.8 constant_dynamic-slice_fusion.6
  143.4 2.0 fusion.48
  145.4 1.4 fusion.49
  146.7 2.4 convolution_add_fusion.2
  150.2 21.0 %dynamic_update_slice.15 = f32[4,512,4,128]{1,0,3,2:T(4,128)} dynamic-update-slice(f32[4,512,4,128]{1,0,3,2:T(4,128)} %get-tuple-element.371, f32[1,512,4,128]{1,0,3,2:T(1,128)S(1)} %copy.143, s32[]{:T(128)S(6)} %copy.151, s32[]{:T(128)} %constant.52.clone.1..sunk.1, s32[]{:T(128)} %constant.52.clone.1..sunk.1, s32[]{:T(128)} %constant.52.clone.1..sunk.1) | dynamic-update-slice | bytes 2097156 | tf_op jit(solution)/shard_map/while/body/jit(dynamic_update_index_in_dim)/dynamic_update_slice | solution.py:73
  171.3 1.3 bitcast_dynamic-update-slice_fusion.2
  175.9 1.8 constant_dynamic-slice_fusion.6
  177.6 2.0 fusion.48
  179.6 1.4 fusion.49
  181.0 2.4 convolution_add_fusion.2
  184.5 21.0 %dynamic_update_slice.15 = f32[4,512,4,128]{1,0,3,2:T(4,128)} dynamic-update-slice(f32[4,512,4,128]{1,0,3,2:T(4,128)} %get-tuple-element.371, f32[1,512,4,128]{1,0,3,2:T(1,128)S(1)} %copy.143, s32[]{:T(128)S(6)} %copy.151, s32[]{:T(128)} %constant.52.clone.1..sunk.1, s32[]{:T(128)} %constant.52.clone.1..sunk.1, s32[]{:T(128)} %constant.52.clone.1..sunk.1) | dynamic-update-slice | bytes 2097156 | tf_op jit(solution)/shard_map/while/body/jit(dynamic_update_index_in_dim)/dynamic_update_slice | solution.py:73
  205.5 1.3 bitcast_dynamic-update-slice_fusion.2
  210.1 1.8 constant_dynamic-slice_fusion.6
  211.9 2.0 fusion.48
  213.9 1.4 fusion.49
  215.2 2.4 convolution_add_fusion.2
  218.7 21.0 %dynamic_update_slice.15 = f32[4,512,4,128]{1,0,3,2:T(4,128)} dynamic-update-slice(f32[4,512,4,128]{1,0,3,2:T(4,128)} %get-tuple-element.371, f32[1,512,4,128]{1,0,3,2:T(1,128)S(1)} %copy.143, s32[]{:T(128)S(6)} %copy.151, s32[]{:T(128)} %constant.52.clone.1..sunk.1, s32[]{:T(128)} %constant.52.clone.1..sunk.1, s32[]{:T(128)} %constant.52.clone.1..sunk.1) | dynamic-update-slice | bytes 2097156 | tf_op jit(solution)/shard_map/while/body/jit(dynamic_update_index_in_dim)/dynamic_update_slice | solution.py:73
  239.8 1.3 bitcast_dynamic-update-slice_fusion.2
  241.4 9.8 %convolution_convert_fusion.2 = bf16[2048,512]{1,0:T(8,128)(2,1)} fusion(bf16[2048,2048]{1,0:T(8,128)(2,1)} %all-gather.4.cloned.1.call-done, bf16[2048,512]{1,0:T(8,128)(2,1)} %param.16), kind=kOutput, calls=%fused_computation.50 | convolution fusion | flops 4296015872 | bytes 12582912 | tf_op jit(solution)/shard_map/dot_general | solution.py:95
  251.2 4.4 %all-to-all-start = ((bf16[4,512,512]{2,1,0:T(8,128)(2,1)}), bf16[4,512,512]{2,1,0:T(8,128)(2,1)}, u32[]{:S(2)}, u32[]{:S(2)}) async-start(bf16[4,512,512]{2,1,0:T(8,128)(2,1)} %bitcast.2), calls=%async_computation | async-start | bytes 4194304 | tf_op jit(solution)/shard_map/all_to_all | solution.py:119
  255.7 4.9 %all-reduce = bf16[8]{0:T(256)(128)(2,1)S(1)} all-reduce(bf16[8]{0:T(256)(128)(2,1)S(1)} %dynamic-update-slice), channel_id=2, replica_groups=mesh['seq'=2,'mp'=4,'dp'=4] {'seq'}, use_global_device_ids=true, to_apply=%add | all-reduce | flops 8 | bytes 32
  260.7 5.7 %all-gather.1 = bf16[8,128,128]{2,1,0:T(8,128)(2,1)S(1)} all-gather(bf16[4,128,128]{2,1,0:T(8,128)(2,1)S(1)} %convert_element_type.89), channel_id=3, replica_groups=mesh['seq'=2,'mp'=4,'dp'=4] {'seq'}, dimensions={0}, use_global_device_ids=true | all-gather | bytes 393216 | tf_op jit(solution)/shard_map/all_gather | solution.py:12
  266.4 6.1 %reshape.91 = f32[2048,4,128]{0,2,1:T(8,128)} reshape(f32[4,512,4,128]{1,0,3,2:T(4,128)} %get-tuple-element.107) | data formatting | bytes 8388608 | tf_op jit(solution)/shard_map/reshape | solution.py:76
  272.5 8.8 %fusion.24 = bf16[2048,4,128]{0,2,1:T(8,128)(2,1)} fusion(f32[2048,4,128]{0,2,1:T(8,128)} %reshape.91, f32[4,128,128]{2,1,0:T(8,128)S(1)} %get-tuple-element.110, f32[2048,4,128]{2,0,1:T(8,128)} %bitcast.128), kind=kOutput, calls=%fused_computation.43 | convolution fusion | flops 1612709888 | bytes 10747904 | tf_op jit(solution)/shard_map/tha,hab->thb/dot_general | solution.py:113
  281.4 3.3 all_to_all.22
  284.7 1.7 copy.79
  286.4 3.6 %all-to-all-start.1 = ((bf16[4,512,512]{1,2,0:T(8,128)(2,1)}), bf16[4,512,512]{1,2,0:T(8,128)(2,1)S(1)}, u32[]{:S(2)}, u32[]{:S(2)}) async-start(bf16[4,512,512]{1,2,0:T(8,128)(2,1)} %copy.79), calls=%async_computation.1 | async-start | bytes 4194304 | tf_op jit(solution)/shard_map/all_to_all | solution.py:118
  290.0 2.2 convert_bitcast_fusion
  292.2 2.6 copy.94
  294.8 20.9 %all-to-all-done.1 = bf16[4,512,512]{1,2,0:T(8,128)(2,1)S(1)} async-done(((bf16[4,512,512]{1,2,0:T(8,128)(2,1)}), bf16[4,512,512]{1,2,0:T(8,128)(2,1)S(1)}, u32[]{:S(2)}, u32[]{:S(2)}) %all-to-all-start.1) | async-done | bytes 2097184 | tf_op jit(solution)/shard_map/all_to_all | solution.py:118
  316.2 2.6 convert_element_type.105
  318.8 5.4 %copy.80 = f32[512,2048]{1,0:T(8,128)} copy(f32[512,2048]{0,1:T(8,128)} %bitcast.127) | data formatting | bytes 8388608 | tf_op jit(solution)/shard_map/convert_element_type | solution.py:121
  324.2 6.4 %multiply_convert_fusion.1 = bf16[512,2048]{1,0:T(8,128)(2,1)} fusion(f32[512,2048]{1,0:T(8,128)} %copy.80, f32[512,2048]{1,0:T(8,128)} %bitcast.126, f32[2048]{0:T(1024)S(1)} %copy-done.3, f32[512]{0:T(512)S(1)} %add_rsqrt_fusion), kind=kLoop, calls=%fused_computation.45 | loop fusion | flops 8388608 | bytes 10496000 | tf_op jit(solution)/shard_map/convert_element_type | solution.py:129
  (84 shorter events, 20.5 us)
Async XLA Ops:
  6.5 63.4 %copy-start = (bf16[2048,512]{1,0:T(8,128)(2,1)S(1)}, bf16[2048,512]{1,0:T(8,128)(2,1)}, u32[]{:S(2)}) copy-start(bf16[2048,512]{1,0:T(8,128)(2,1)} %param.13) | copy-start | bytes 6291460
  6.5 63.4 %all-gather.4.cloned.1.call-start = ((), (), s32[]{:S(2)}) async-start(), calls=%async_computation.2 | async-start | bytes 10485760 | tf_op jit(solution)/shard_map/all_gather | solution.py:92
  107.4 1.8 copy-start.2
  141.6 1.8 copy-start.2
  175.9 1.8 copy-start.2
  210.1 1.8 copy-start.2
  251.2 35.2 %all-to-all-start = ((bf16[4,512,512]{2,1,0:T(8,128)(2,1)}), bf16[4,512,512]{2,1,0:T(8,128)(2,1)}, u32[]{:S(2)}, u32[]{:S(2)}) async-start(bf16[4,512,512]{2,1,0:T(8,128)(2,1)} %bitcast.2), calls=%async_computation | async-start | bytes 4194304 | tf_op jit(solution)/shard_map/all_to_all | solution.py:119
  286.4 29.3 %all-to-all-start.1 = ((bf16[4,512,512]{1,2,0:T(8,128)(2,1)}), bf16[4,512,512]{1,2,0:T(8,128)(2,1)S(1)}, u32[]{:S(2)}, u32[]{:S(2)}) async-start(bf16[4,512,512]{1,2,0:T(8,128)(2,1)} %copy.79), calls=%async_computation.1 | async-start | bytes 4194304 | tf_op jit(solution)/shard_map/all_to_all | solution.py:118
  318.8 5.4 %copy-start.3 = (f32[2048]{0:T(1024)S(1)}, f32[2048]{0:T(1024)}, u32[]{:S(2)}) copy-start(f32[2048]{0:T(1024)} %param.19) | copy-start | bytes 24580
  324.2 6.4 %copy-start.1 = (bf16[2048,512]{1,0:T(8,128)(2,1)S(1)}, bf16[2048,512]{1,0:T(8,128)(2,1)}, u32[]{:S(2)}) copy-start(bf16[2048,512]{1,0:T(8,128)(2,1)} %param.13) | copy-start | bytes 6291460
Sparse Core Ops, SparseCore 0:
  8.9 60.9 all-gather.3
where the time goes:
time: 341 us; the launch traced here: 337 us
  local copies, waits for them, and re-layouts  131 us (38%)
  waiting for transfers between devices  80.8 us (24%)
  matrix products  67.6 us (20%)
  other arithmetic  25.1 us (7%)
  between operations  14.2 us (4%)
  blocking collectives  10.7 us (3%)
  starting transfers between devices  8.06 us (2%)
    dynamic_update_slice x8, local copies, waits for them, and re-layouts, run_blocks(): lax.scan(advance, initial, (shaped(queries), shaped(key_rows), shaped(val...  88.5 us
    all_gather x1, waiting for transfers between devices, body(): piece = lax.all_gather(tokens, 'mp', axis=1, tiled=True)  59.2 us
    dot_general x4, matrix products, body(): results.append(jnp.dot(piece, weight, preferred_element_type=jnp.float32))  35.9 us
    all_to_all x1, waiting for transfers between devices, body(): lax.all_to_all(output, 'mp', split_axis=0, concat_axis=1, tiled=True)  20.9 us
    dynamic_slice x8, local copies, waits for them, and re-layouts, run_blocks(): lax.scan(advance, initial, (shaped(queries), shaped(key_rows), shaped(val...  11.9 us
    dot_general x4, matrix products, advance(): jnp.einsum('sha,shb->hab', key_scaled, value_blk.astype(jnp.float32), pre...  9.56 us
    dot_general x1, matrix products, body(): jnp.einsum('tha,hab->thb', query_device, incoming, precision=lax.Precisio...  8.83 us
    reshape x3, local copies, waits for them, and re-layouts, shaped(): return source.reshape(block_count, block_rows, head_count, head_width)  8.09 us
  transfers between devices with their start and end apart: 3, of which 2 were waited for; matrix products, arithmetic and copies ran while one was open for 7% of the time, Pallas kernels for 0%

commit v1 on v0

--- a/solution.py
+++ b/solution.py
@@ -4,6 +4,12 @@
 from jax.sharding import PartitionSpec as P
 
 DH = 128
+
+
+def all_parts(array, axis, dim):
+    parts = lax.all_gather(array, axis, axis=0, tiled=False)
+    result = jnp.concatenate(parts, axis=dim)
+    return result
 
 
 def carried_in(shard, axis, join, neutral):
@@ -89,7 +95,7 @@
     head_width = local_width // head_count
     empty = jnp.zeros((seq_rows, local_width), jnp.float32)
     summed = (empty, empty, empty, empty)
-    piece = lax.all_gather(tokens, "mp", axis=1, tiled=True)
+    piece = all_parts(tokens, "mp", 1)
     results = []
     for weight, partial_value in zip((w_query, w_key, w_value, w_gate), summed):
         results.append(jnp.dot(piece, weight, preferred_element_type=jnp.float32))

time: 341 us -> 353 us (1.035)
  local copies, waits for them, and re-layouts: 131 us -> 142 us
    reshape x4 -> x5, local copies, waits for them, and re-layouts: 0.07 us -> 11.5 us  [the longest x1 11.4 us: all_parts(): result = jnp.concatenate(parts, axis=dim)]
where the time goes in v1:
time: 353 us; the launch traced here: 349 us
  local copies, waits for them, and re-layouts  142 us (40%)
  waiting for transfers between devices  80.8 us (23%)
  matrix products  68 us (19%)
  other arithmetic  25.1 us (7%)
  between operations  14.2 us (4%)
  blocking collectives  10.7 us (3%)
  starting transfers between devices  8.07 us (2%)
    dynamic_update_slice x8, local copies, waits for them, and re-layouts, run_blocks(): lax.scan(advance, initial, (shaped(queries), shaped(key_rows), shaped(val...  88.4 us
    all_gather x1, waiting for transfers between devices, all_parts(): parts = lax.all_gather(array, axis, axis=0, tiled=False)  59.2 us
    dot_general x4, matrix products, body(): results.append(jnp.dot(piece, weight, preferred_element_type=jnp.float32))  36.3 us
    all_to_all x1, waiting for transfers between devices, body(): lax.all_to_all(output, 'mp', split_axis=0, concat_axis=1, tiled=True)  20.9 us
    dynamic_slice x8, local copies, waits for them, and re-layouts, run_blocks(): lax.scan(advance, initial, (shaped(queries), shaped(key_rows), shaped(val...  11.9 us
    reshape x1, local copies, waits for them, and re-layouts, all_parts(): result = jnp.concatenate(parts, axis=dim)  11.4 us
    dot_general x4, matrix products, advance(): jnp.einsum('sha,shb->hab', key_scaled, value_blk.astype(jnp.float32), pre...  9.56 us
    dot_general x1, matrix products, body(): jnp.einsum('tha,hab->thb', query_device, incoming, precision=lax.Precisio...  8.83 us
  transfers between devices with their start and end apart: 3, of which 2 were waited for; matrix products, arithmetic and copies ran while one was open for 7% of the time, Pallas kernels for 0%

profile of v1, /device:TPU:0, one launch (start us, length us, event | category | flops | bytes accessed | tf_op | source)
XLA Modules:
  0.0 349.3 jit_solution(14921024207149176118)
XLA Ops:
  10.7 59.2 %all-gather.5.cloned.1.call-done = bf16[8192,512]{1,0:T(8,128)(2,1)} async-done(((bf16[2048,512]{1,0:T(8,128)(2,1)}), bf16[8192,512]{1,0:T(8,128)(2,1)}) %all-gather.5.cloned.1.call-update) | async-done | bytes 8388624 | tf_op jit(solution)/shard_map/all_gather | solution.py:10
  69.9 11.4 %copy.90 = bf16[2048,4,512]{0,2,1:T(8,128)(2,1)} copy(bf16[2048,4,512]{2,0,1:T(8,128)(2,1)} %bitcast.132) | data formatting | bytes 16777216 | tf_op jit(solution)/shard_map/reshape | solution.py:11
  81.3 9.4 %convolution_convert_fusion = bf16[2048,512]{1,0:T(8,128)(2,1)} fusion(bf16[2048,2048]{0,1:T(8,128)(2,1)} %bitcast.133, bf16[2048,512]{1,0:T(8,128)(2,1)S(1)} %copy-done), kind=kOutput, calls=%fused_computation.48 | convolution fusion | flops 4296015872 | bytes 12582912 | tf_op jit(solution)/shard_map/dot_general | solution.py:101
  90.7 4.0 %reshape.98 = bf16[4,512,4,128]{3,2,1,0:T(4,128)(2,1)} reshape(bf16[2048,512]{1,0:T(8,128)(2,1)} %convolution_convert_fusion) | data formatting | bytes 4194304 | tf_op jit(solution)/shard_map/reshape | solution.py:41
  94.7 8.5 %convolution_convert_fusion.1 = bf16[2048,512]{1,0:T(8,128)(2,1)S(1)} fusion(bf16[2048,2048]{0,1:T(8,128)(2,1)} %bitcast.134, bf16[2048,512]{1,0:T(8,128)(2,1)} %param.15), kind=kOutput, calls=%fused_computation.49 | convolution fusion | flops 4296015872 | bytes 12582912 | tf_op jit(solution)/shard_map/dot_general | solution.py:101
  103.2 2.1 reshape.97
  105.3 8.7 %multiply_convert_fusion.2 = bf16[2048,512]{1,0:T(8,128)(2,1)S(1)} fusion(bf16[2048,2048]{0,1:T(8,128)(2,1)} %bitcast.135, bf16[2048,512]{1,0:T(8,128)(2,1)} %param.14), kind=kOutput, calls=%fused_computation.47 | convolution fusion | flops 4297064448 | bytes 12582912 | tf_op jit(solution)/shard_map/dot_general | solution.py:101
  114.0 9.7 %convolution_convert_fusion.2 = bf16[2048,512]{1,0:T(8,128)(2,1)} fusion(bf16[2048,2048]{0,1:T(8,128)(2,1)} %bitcast.136, bf16[2048,512]{1,0:T(8,128)(2,1)S(1)} %copy-done.4), kind=kOutput, calls=%fused_computation.50 | convolution fusion | flops 4296015872 | bytes 12582912 | tf_op jit(solution)/shard_map/dot_general | solution.py:101
  123.7 2.0 reshape.96
  125.7 136.8 %while.31 = (s32[]{:T(128)}, f32[4,128,128]{2,1,0:T(8,128)S(1)}, f32[4]{0:T(128)S(1)}, f32[4,512,4,128]{1,0,3,2:T(4,128)}, f32[4,512,4,128]{3,1,0,2:T(8,128)}, /...) while((s32[]{:T(128)}, f32[4,128,128]{2,1,0:T(8,128)S(1)}, ...), condition=%wide.region_3.4_spmd.clone.clone, body=%wide.region_0.3_spmd.clone.clone.sunk | while | flops 1350045696 | bytes 18760368 | solution.py:79
  129.0 1.8 constant_dynamic-slice_fusion.6
  130.8 2.0 fusion.48
  132.7 1.4 fusion.49
  134.1 2.4 convolution_add_fusion.2
  137.6 21.0 %dynamic_update_slice.15 = f32[4,512,4,128]{1,0,3,2:T(4,128)} dynamic-update-slice(f32[4,512,4,128]{1,0,3,2:T(4,128)} %get-tuple-element.380, f32[1,512,4,128]{1,0,3,2:T(1,128)S(1)} %copy.163, s32[]{:T(128)S(6)} %copy.171, s32[]{:T(128)} %constant.52.clone.1..sunk.1, s32[]{:T(128)} %constant.52.clone.1..sunk.1, s32[]{:T(128)} %constant.52.clone.1..sunk.1) | dynamic-update-slice | bytes 2097156 | tf_op jit(solution)/shard_map/while/body/jit(dynamic_update_index_in_dim)/dynamic_update_slice | solution.py:79
  158.6 1.4 bitcast_dynamic-update-slice_fusion.2
  163.2 1.8 constant_dynamic-slice_fusion.6
  165.0 2.0 fusion.48
  167.0 1.4 fusion.49
  168.3 2.4 convolution_add_fusion.2
  171.8 21.0 %dynamic_update_slice.15 = f32[4,512,4,128]{1,0,3,2:T(4,128)} dynamic-update-slice(f32[4,512,4,128]{1,0,3,2:T(4,128)} %get-tuple-element.380, f32[1,512,4,128]{1,0,3,2:T(1,128)S(1)} %copy.163, s32[]{:T(128)S(6)} %copy.171, s32[]{:T(128)} %constant.52.clone.1..sunk.1, s32[]{:T(128)} %constant.52.clone.1..sunk.1, s32[]{:T(128)} %constant.52.clone.1..sunk.1) | dynamic-update-slice | bytes 2097156 | tf_op jit(solution)/shard_map/while/body/jit(dynamic_update_index_in_dim)/dynamic_update_slice | solution.py:79
  192.8 1.3 bitcast_dynamic-update-slice_fusion.2
  197.5 1.8 constant_dynamic-slice_fusion.6
  199.2 2.0 fusion.48
  201.2 1.4 fusion.49
  202.6 2.4 convolution_add_fusion.2
  206.1 21.0 %dynamic_update_slice.15 = f32[4,512,4,128]{1,0,3,2:T(4,128)} dynamic-update-slice(f32[4,512,4,128]{1,0,3,2:T(4,128)} %get-tuple-element.380, f32[1,512,4,128]{1,0,3,2:T(1,128)S(1)} %copy.163, s32[]{:T(128)S(6)} %copy.171, s32[]{:T(128)} %constant.52.clone.1..sunk.1, s32[]{:T(128)} %constant.52.clone.1..sunk.1, s32[]{:T(128)} %constant.52.clone.1..sunk.1) | dynamic-update-slice | bytes 2097156 | tf_op jit(solution)/shard_map/while/body/jit(dynamic_update_index_in_dim)/dynamic_update_slice | solution.py:79
  227.1 1.3 bitcast_dynamic-update-slice_fusion.2
  231.6 1.8 constant_dynamic-slice_fusion.6
  233.4 2.0 fusion.48
  235.4 1.4 fusion.49
  236.8 2.4 convolution_add_fusion.2
  240.2 21.0 %dynamic_update_slice.15 = f32[4,512,4,128]{1,0,3,2:T(4,128)} dynamic-update-slice(f32[4,512,4,128]{1,0,3,2:T(4,128)} %get-tuple-element.380, f32[1,512,4,128]{1,0,3,2:T(1,128)S(1)} %copy.163, s32[]{:T(128)S(6)} %copy.171, s32[]{:T(128)} %constant.52.clone.1..sunk.1, s32[]{:T(128)} %constant.52.clone.1..sunk.1, s32[]{:T(128)} %constant.52.clone.1..sunk.1) | dynamic-update-slice | bytes 2097156 | tf_op jit(solution)/shard_map/while/body/jit(dynamic_update_index_in_dim)/dynamic_update_slice | solution.py:79
  261.2 1.3 bitcast_dynamic-update-slice_fusion.2
  262.8 4.5 %all-to-all-start = ((bf16[4,512,512]{2,1,0:T(8,128)(2,1)}), bf16[4,512,512]{2,1,0:T(8,128)(2,1)}, u32[]{:S(2)}, u32[]{:S(2)}) async-start(bf16[4,512,512]{2,1,0:T(8,128)(2,1)} %bitcast.139), calls=%async_computation | async-start | bytes 4194304 | tf_op jit(solution)/shard_map/all_to_all | solution.py:125
  267.3 4.9 %all-reduce = bf16[8]{0:T(256)(128)(2,1)S(1)} all-reduce(bf16[8]{0:T(256)(128)(2,1)S(1)} %dynamic-update-slice), channel_id=3, replica_groups=mesh['seq'=2,'mp'=4,'dp'=4] {'seq'}, use_global_device_ids=true, to_apply=%add | all-reduce | flops 8 | bytes 32
  272.3 5.7 %all-gather.2 = bf16[8,128,128]{2,1,0:T(8,128)(2,1)S(1)} all-gather(bf16[4,128,128]{2,1,0:T(8,128)(2,1)S(1)} %convert_element_type.89), channel_id=4, replica_groups=mesh['seq'=2,'mp'=4,'dp'=4] {'seq'}, dimensions={0}, use_global_device_ids=true | all-gather | bytes 393216 | tf_op jit(solution)/shard_map/all_gather | solution.py:18
  278.1 6.1 %reshape.99 = f32[2048,4,128]{0,2,1:T(8,128)} reshape(f32[4,512,4,128]{1,0,3,2:T(4,128)} %get-tuple-element.107) | data formatting | bytes 8388608 | tf_op jit(solution)/shard_map/reshape | solution.py:82
  284.4 8.8 %fusion.24 = bf16[2048,4,128]{0,2,1:T(8,128)(2,1)} fusion(f32[2048,4,128]{0,2,1:T(8,128)} %reshape.99, f32[4,128,128]{2,1,0:T(8,128)S(1)} %get-tuple-element.110, f32[2048,4,128]{2,0,1:T(8,128)} %bitcast.137), kind=kOutput, calls=%fused_computation.43 | convolution fusion | flops 1612709888 | bytes 10747904 | tf_op jit(solution)/shard_map/tha,hab->thb/dot_general | solution.py:119
  293.2 3.3 all_to_all.22
  296.5 1.7 copy.99
  298.3 3.6 %all-to-all-start.1 = ((bf16[4,512,512]{1,2,0:T(8,128)(2,1)}), bf16[4,512,512]{1,2,0:T(8,128)(2,1)S(1)}, u32[]{:S(2)}, u32[]{:S(2)}) async-start(bf16[4,512,512]{1,2,0:T(8,128)(2,1)} %copy.99), calls=%async_computation.1 | async-start | bytes 4194304 | tf_op jit(solution)/shard_map/all_to_all | solution.py:124
  301.9 2.2 convert_bitcast_fusion
  304.1 2.6 copy.114
  306.6 20.9 %all-to-all-done.1 = bf16[4,512,512]{1,2,0:T(8,128)(2,1)S(1)} async-done(((bf16[4,512,512]{1,2,0:T(8,128)(2,1)}), bf16[4,512,512]{1,2,0:T(8,128)(2,1)S(1)}, u32[]{:S(2)}, u32[]{:S(2)}) %all-to-all-start.1) | async-done | bytes 2097184 | tf_op jit(solution)/shard_map/all_to_all | solution.py:124
  328.0 2.6 convert_element_type.105
  330.6 5.4 %copy.100 = f32[512,2048]{1,0:T(8,128)} copy(f32[512,2048]{0,1:T(8,128)} %bitcast.131) | data formatting | bytes 8388608 | tf_op jit(solution)/shard_map/convert_element_type | solution.py:127
  336.0 6.4 %multiply_convert_fusion.1 = bf16[512,2048]{1,0:T(8,128)(2,1)} fusion(f32[512,2048]{1,0:T(8,128)} %copy.100, f32[512,2048]{1,0:T(8,128)} %bitcast.130, f32[2048]{0:T(1024)S(1)} %copy-done.3, f32[512]{0:T(512)S(1)} %add_rsqrt_fusion), kind=kLoop, calls=%fused_computation.45 | loop fusion | flops 8388608 | bytes 10496000 | tf_op jit(solution)/shard_map/convert_element_type | solution.py:135
  (87 shorter events, 21.9 us)
Async XLA Ops:
  6.5 74.8 %copy-start = (bf16[2048,512]{1,0:T(8,128)(2,1)S(1)}, bf16[2048,512]{1,0:T(8,128)(2,1)}, u32[]{:S(2)}) copy-start(bf16[2048,512]{1,0:T(8,128)(2,1)} %param.13) | copy-start | bytes 6291460
  6.5 63.4 %all-gather.5.cloned.1.call-start = ((), (), s32[]{:S(2)}) async-start(), calls=%async_computation.2 | async-start | bytes 10485760 | tf_op jit(solution)/shard_map/all_gather | solution.py:10
  105.3 8.7 %copy-start.4 = (bf16[2048,512]{1,0:T(8,128)(2,1)S(1)}, bf16[2048,512]{1,0:T(8,128)(2,1)}, u32[]{:S(2)}) copy-start(bf16[2048,512]{1,0:T(8,128)(2,1)} %param.16) | copy-start | bytes 6291460
  129.0 1.8 copy-start.2
  163.2 1.8 copy-start.2
  197.4 1.8 copy-start.2
  231.6 1.8 copy-start.2
  262.8 35.5 %all-to-all-start = ((bf16[4,512,512]{2,1,0:T(8,128)(2,1)}), bf16[4,512,512]{2,1,0:T(8,128)(2,1)}, u32[]{:S(2)}, u32[]{:S(2)}) async-start(bf16[4,512,512]{2,1,0:T(8,128)(2,1)} %bitcast.139), calls=%async_computation | async-start | bytes 4194304 | tf_op jit(solution)/shard_map/all_to_all | solution.py:125
  298.3 29.3 %all-to-all-start.1 = ((bf16[4,512,512]{1,2,0:T(8,128)(2,1)}), bf16[4,512,512]{1,2,0:T(8,128)(2,1)S(1)}, u32[]{:S(2)}, u32[]{:S(2)}) async-start(bf16[4,512,512]{1,2,0:T(8,128)(2,1)} %copy.99), calls=%async_computation.1 | async-start | bytes 4194304 | tf_op jit(solution)/shard_map/all_to_all | solution.py:124
  330.6 5.4 %copy-start.3 = (f32[2048]{0:T(1024)S(1)}, f32[2048]{0:T(1024)}, u32[]{:S(2)}) copy-start(f32[2048]{0:T(1024)} %param.19) | copy-start | bytes 24580
  336.0 6.4 %copy-start.1 = (bf16[2048,512]{1,0:T(8,128)(2,1)S(1)}, bf16[2048,512]{1,0:T(8,128)(2,1)}, u32[]{:S(2)}) copy-start(bf16[2048,512]{1,0:T(8,128)(2,1)} %param.13) | copy-start | bytes 6291460
Sparse Core Ops, SparseCore 0:
  8.9 60.9 all-gather.4
